TPU v7x, 32 devices: a whole 2x2x4 slice. The times are simulated.
32 devices in a mesh: row: 4 (over x, core), col: 4 (over z), depth: 2 (over y).
Axes of the slice: x: 2, y: 2, z: 4, core: 2. Of those that a mesh axis runs over, the one named last changes fastest.
Arguments:
- tokens: bfloat16 [512, 4096], P(('col', 'depth'), 'row'), may hold values from -6 to 6
- w_gate: bfloat16 [4096, 14336], P('row', 'col'), may hold values from -0.09375 to 0.09375
- w_up: bfloat16 [4096, 14336], P('row', 'col'), may hold values from -0.09375 to 0.09375
- w_down: bfloat16 [14336, 4096], P('col', 'row'), may hold values from -0.046875 to 0.046875
- cotangent: bfloat16 [512, 4096], P(('col', 'depth'), 'row'), may hold values from -0.25 to 0.25
Outputs:
- mixed: bfloat16 [512, 4096], P(('col', 'depth'), 'row')
- grad_gate: bfloat16 [4096, 14336], P(('row', 'depth'), 'col')
- grad_up: bfloat16 [4096, 14336], P(('row', 'depth'), 'col')
- grad_down: bfloat16 [14336, 4096], P(('col', 'depth'), 'row')
All inputs are finite; a program needn't handle non-finite values.
Results may differ from a plain program's by a relative error of at most 0.025.
Values may be sent and summed in bfloat16 or wider, within the bound.
A program may use at most 128 MiB of HBM per device.

v0:
```python
import jax
import jax.numpy as jnp
from jax import lax
from jax.sharding import PartitionSpec as P

COLS_CONTRACT = (((1,), (1,)), ((), ()))
ROWS_CONTRACT = (((0,), (0,)), ((), ()))


def gate_grads(hidden_grad, gate_sum, up_sum):
    sigmoid_gate = jax.nn.sigmoid(gate_sum)
    d_gate = (hidden_grad * up_sum * sigmoid_gate * (1.0 + gate_sum * (1.0 - sigmoid_gate))).astype(
        jnp.bfloat16
    )
    d_up = (hidden_grad * gate_sum * sigmoid_gate).astype(jnp.bfloat16)
    return (d_gate, d_up)


def per_device(tokens, w_gate, w_up, w_down, cotangent):
    hid_width = w_gate.shape[1]
    token_rows = lax.all_gather(tokens, "col", axis=0, tiled=True)
    row_piece = token_rows
    joined = lax.psum_scatter(
        jnp.concatenate(
            [
                jnp.dot(row_piece, w_gate, preferred_element_type=jnp.float32),
                jnp.dot(row_piece, w_up, preferred_element_type=jnp.float32),
            ],
            axis=1,
        ).astype(jnp.bfloat16),
        "row",
        scatter_dimension=0,
        tiled=True,
    ).astype(jnp.float32)
    gate_sum = joined[:, :hid_width]
    up_sum = joined[:, hid_width:]
    hidden = (jax.nn.silu(gate_sum) * up_sum).astype(jnp.bfloat16)
    hidden_rows = lax.all_gather(hidden, "row", axis=0, tiled=True)
    row_piece = hidden_rows
    mixed = lax.psum_scatter(
        jnp.dot(row_piece, w_down, preferred_element_type=jnp.float32).astype(jnp.bfloat16),
        "col",
        scatter_dimension=0,
        tiled=True,
    )
    cot_rows = lax.all_gather(cotangent, "col", axis=0, tiled=True)
    row_piece = cot_rows
    hidden_grad = lax.psum_scatter(
        lax.dot_general(
            row_piece, w_down, COLS_CONTRACT, preferred_element_type=jnp.float32
        ).astype(jnp.bfloat16),
        "row",
        scatter_dimension=0,
        tiled=True,
    ).astype(jnp.float32)
    d_gate, d_up = gate_grads(hidden_grad, gate_sum, up_sum)
    d_gate_rows, d_up_rows = (
        lax.all_gather(d_gate, "row", axis=0, tiled=True),
        lax.all_gather(d_up, "row", axis=0, tiled=True),
    )
    down_term = lax.dot_general(
        hidden_rows, cot_rows, ROWS_CONTRACT, preferred_element_type=jnp.float32
    )
    grad_down = lax.psum_scatter(
        down_term.astype(jnp.bfloat16), "depth", scatter_dimension=0, tiled=True
    )
    layer_tokens = lax.all_to_all(token_rows, "depth", split_axis=1, concat_axis=0, tiled=True)
    block_rows = token_rows.shape[0]
    empty_grad = jnp.zeros((layer_tokens.shape[1], d_gate_rows.shape[1]), jnp.float32)
    first_row = jnp.int32(0)
    gate_total = empty_grad
    up_total = empty_grad
    gate_piece = lax.all_gather(d_gate_rows, "depth", axis=0, tiled=True)
    up_piece = lax.all_gather(d_up_rows, "depth", axis=0, tiled=True)
    for sub_index in range(gate_piece.shape[0] // block_rows):
        gate_block = gate_piece[sub_index * block_rows : (sub_index + 1) * block_rows]
        up_block = up_piece[sub_index * block_rows : (sub_index + 1) * block_rows]
        offset = first_row + sub_index * block_rows
        tok_block = lax.dynamic_slice_in_dim(layer_tokens, offset, block_rows, 0)
        gate_part = lax.optimization_barrier(
            lax.dot_general(
                tok_block, gate_block, ROWS_CONTRACT, preferred_element_type=jnp.float32
            ).astype(jnp.bfloat16)
        )
        up_part = lax.optimization_barrier(
            lax.dot_general(
                tok_block, up_block, ROWS_CONTRACT, preferred_element_type=jnp.float32
            ).astype(jnp.bfloat16)
        )
        gate_total = gate_total + gate_part.astype(jnp.float32)
        up_total = up_total + up_part.astype(jnp.float32)
    return (mixed, gate_total.astype(jnp.bfloat16), up_total.astype(jnp.bfloat16), grad_down)


def solution(mesh):
    placed = (
        P(("col", "depth"), "row"),
        P("row", "col"),
        P("row", "col"),
        P("col", "row"),
        P(("col", "depth"), "row"),
    )
    return jax.shard_map(
        per_device,
        mesh=mesh,
        in_specs=placed,
        out_specs=(
            P(("col", "depth"), "row"),
            P(("row", "depth"), "col"),
            P(("row", "depth"), "col"),
            P(("col", "depth"), "row"),
        ),
        check_vma=False,
    )
```

profile of v0, /device:TPU:0, one launch (start us, length us, event | category | flops | bytes accessed | tf_op | source)
XLA Modules:
  0.0 411.8 jit_solution(894660631228663583)
XLA Ops:
  7.2 0.0 reduce-scatter.5.cloned.1.call-start
  7.2 0.0 slice-start
  7.2 17.7 %all_gather.21 = bf16[256,1024]{1,0:T(8,128)(2,1)S(1)} all-gather(bf16[64,1024]{1,0:T(8,128)(2,1)} %param.5), channel_id=1, replica_groups=mesh['row'=4,'col'=4,'depth'=2] {'col'}, dimensions={0}, use_global_device_ids=true | all-gather | bytes 655360 | tf_op jit(solution)/shard_map/all_gather | solution.py:21
  24.9 0.0 slice-start.1
  24.9 5.3 %convolution_convert_fusion.6 = bf16[256,3584]{1,0:T(8,128)(2,1)S(1)} fusion(bf16[256,1024]{1,0:T(8,128)(2,1)S(1)} %all_gather.21, bf16[1024,3584]{1,0:T(8,128)(2,1)} %param.7), kind=kOutput, calls=%fused_computation.12 | convolution fusion | flops 1879965696 | bytes 9699328 | tf_op jit(solution)/shard_map/dot_general | solution.py:27
  30.2 0.0 slice-done
  30.2 0.0 slice-done.1
  30.3 2.1 convolution_convert_fusion.7
  32.4 2.3 pad_maximum_fusion
  34.6 0.0 copy-start.3
  34.6 0.0 reduce-scatter.5.cloned.1.call-update
  34.6 0.0 reduce-scatter.9.cloned.1.call-start
  34.7 0.8 copy-done.3
  35.5 16.2 %all_gather.23 = bf16[256,1024]{1,0:T(8,128)(2,1)S(1)} all-gather(bf16[64,1024]{1,0:T(8,128)(2,1)S(1)} %copy-done.3), channel_id=1, replica_groups=mesh['row'=4,'col'=4,'depth'=2] {'col'}, dimensions={0}, use_global_device_ids=true | all-gather | bytes 655360 | tf_op jit(solution)/shard_map/all_gather | solution.py:46
  51.8 6.5 %convolution_convert_fusion.5 = bf16[256,3584]{1,0:T(8,128)(2,1)} fusion(bf16[256,1024]{1,0:T(8,128)(2,1)S(1)} %all_gather.23, bf16[3584,1024]{1,0:T(8,128)(2,1)} %param.8), kind=kOutput, calls=%fused_computation.11 | convolution fusion | flops 1879965696 | bytes 9699328 | tf_op jit(solution)/shard_map/dot_general | solution.py:49
  58.3 0.0 reduce-scatter.9.cloned.1.call-update
  58.3 0.0 all-gather.8.cloned.1.call-start
  58.3 19.4 %reduce-scatter.5.cloned.1.call-done = bf16[64,7168]{1,0:T(8,128)(2,1)} async-done(((bf16[256,7168]{1,0:T(8,128)(2,1)}), bf16[64,7168]{1,0:T(8,128)(2,1)}) %reduce-scatter.5.cloned.1.call-update) | async-done | bytes 917520 | tf_op jit(solution)/shard_map/reduce_scatter | solution.py:23
  77.8 1.3 convert_element_type.67
  79.1 31.5 %reduce-scatter.9.cloned.1.call-done = bf16[64,3584]{1,0:T(8,128)(2,1)} async-done(((bf16[256,3584]{1,0:T(8,128)(2,1)}), bf16[64,3584]{1,0:T(8,128)(2,1)}) %reduce-scatter.9.cloned.1.call-update) | async-done | bytes 458768 | tf_op jit(solution)/shard_map/reduce_scatter | solution.py:48
  110.5 2.5 fusion.12
  113.1 0.0 all-gather.8.cloned.1.call-update
  113.1 0.0 all-gather.12.cloned.1.call-start
  113.1 0.5 all-gather.12.cloned.1.call-update
  113.7 0.0 all-gather.6.cloned.1.call-start
  113.7 0.5 all-gather.6.cloned.1.call-update
  114.3 0.0 all-gather.10.cloned.1.call-start
  114.3 20.0 %all-gather.8.cloned.1.call-done = bf16[256,3584]{1,0:T(8,128)(2,1)} async-done(((bf16[64,3584]{1,0:T(8,128)(2,1)}), bf16[256,3584]{1,0:T(8,128)(2,1)}) %all-gather.8.cloned.1.call-update) | async-done | bytes 1835024 | tf_op jit(solution)/shard_map/all_gather | solution.py:58
  134.3 0.0 all-gather.10.cloned.1.call-update
  134.4 0.0 all-gather.14.cloned.1.call-start
  134.4 23.1 %all-gather.12.cloned.1.call-done = bf16[256,3584]{1,0:T(8,128)(2,1)} async-done(((bf16[64,3584]{1,0:T(8,128)(2,1)}), bf16[256,3584]{1,0:T(8,128)(2,1)}) %all-gather.12.cloned.1.call-update) | async-done | bytes 1835024 | tf_op jit(solution)/shard_map/all_gather | solution.py:59
  157.5 0.0 all-gather.14.cloned.1.call-update
  157.5 0.0 reduce-scatter.7.cloned.1.call-start
  157.5 23.0 %all-gather.6.cloned.1.call-done = bf16[256,3584]{1,0:T(8,128)(2,1)} async-done(((bf16[64,3584]{1,0:T(8,128)(2,1)}), bf16[256,3584]{1,0:T(8,128)(2,1)}) %all-gather.6.cloned.1.call-update) | async-done | bytes 1835024 | tf_op jit(solution)/shard_map/all_gather | solution.py:38
  180.6 0.0 copy-start.2
  180.6 6.6 %convolution_convert_fusion.8 = bf16[256,1024]{1,0:T(8,128)(2,1)} fusion(bf16[256,3584]{1,0:T(8,128)(2,1)} %all-gather.6.cloned.1.call-done, bf16[3584,1024]{1,0:T(8,128)(2,1)} %param.8), kind=kOutput, calls=%fused_computation.19 | convolution fusion | flops 1879310336 | bytes 9699328 | tf_op jit(solution)/shard_map/dot_general | solution.py:41
  187.2 0.0 reduce-scatter.7.cloned.1.call-update
  187.2 0.0 reduce-scatter.11.cloned.1.call-start
  187.3 0.0 copy-done.2
  187.3 5.3 %convolution_convert_fusion = bf16[3584,1024]{1,0:T(8,128)(2,1)} fusion(bf16[256,3584]{1,0:T(8,128)(2,1)S(1)} %copy-done.2, bf16[256,1024]{1,0:T(8,128)(2,1)S(1)} %all_gather.23), kind=kOutput, calls=%fused_computation | convolution fusion | flops 1882718208 | bytes 9699328 | tf_op jit(solution)/shard_map/dot_general | solution.py:61
  192.6 0.0 reduce-scatter.11.cloned.1.call-update
  192.6 0.2 copy.18
  192.9 17.3 %all_to_all.16 = bf16[256,2,512]{0,2,1:T(8,128)(2,1)S(1)} all-to-all(bf16[256,2,512]{0,2,1:T(8,128)(2,1)S(1)} %bitcast.36), channel_id=1, replica_groups=mesh['row'=4,'col'=4,'depth'=2] {'depth'}, dimensions={1} | all-to-all | bytes 1048576 | tf_op jit(solution)/shard_map/all_to_all | solution.py:67
  210.2 28.3 %all-gather.10.cloned.1.call-done = bf16[512,3584]{1,0:T(8,128)(2,1)} async-done(((bf16[256,3584]{1,0:T(8,128)(2,1)}), bf16[512,3584]{1,0:T(8,128)(2,1)}) %all-gather.10.cloned.1.call-update) | async-done | bytes 3670032 | tf_op jit(solution)/shard_map/all_gather | solution.py:73
  238.4 0.0 copy-start
  238.4 2.8 fusion
  241.3 0.0 copy-done
  241.3 1.2 fusion.1
  242.5 2.9 add_convert_fusion.1
  245.3 6.1 %copy.21 = bf16[512,3584]{1,0:T(8,128)(2,1)} copy(bf16[512,3584]{0,1:T(8,128)(2,1)} %add_convert_fusion.1) | data formatting | bytes 7340032
  251.5 39.4 %all-gather.14.cloned.1.call-done = bf16[512,3584]{1,0:T(8,128)(2,1)} async-done(((bf16[256,3584]{1,0:T(8,128)(2,1)}), bf16[512,3584]{1,0:T(8,128)(2,1)}) %all-gather.14.cloned.1.call-update) | async-done | bytes 3670032 | tf_op jit(solution)/shard_map/all_gather | solution.py:74
  290.8 0.0 copy-start.1
  290.8 2.8 fusion.2
  293.7 0.0 copy-done.1
  293.7 1.2 fusion.3
  294.9 3.0 add_convert_fusion
  297.8 5.9 %copy.22 = bf16[512,3584]{1,0:T(8,128)(2,1)} copy(bf16[512,3584]{0,1:T(8,128)(2,1)} %add_convert_fusion) | data formatting | bytes 7340032
  303.7 11.8 %reduce-scatter.7.cloned.1.call-done = bf16[64,1024]{1,0:T(8,128)(2,1)} async-done(((bf16[256,1024]{1,0:T(8,128)(2,1)}), bf16[64,1024]{1,0:T(8,128)(2,1)}) %reduce-scatter.7.cloned.1.call-update) | async-done | bytes 131088 | tf_op jit(solution)/shard_map/reduce_scatter | solution.py:40
  315.5 89.7 %reduce-scatter.11.cloned.1.call-done = bf16[1792,1024]{1,0:T(8,128)(2,1)} async-done(((bf16[3584,1024]{1,0:T(8,128)(2,1)}), bf16[1792,1024]{1,0:T(8,128)(2,1)}) %reduce-scatter.11.cloned.1.call-update) | async-done | bytes 3670032 | tf_op jit(solution)/shard_map/reduce_scatter | solution.py:64
  (1 shorter events, 0.0 us)
Async XLA Ops:
  7.2 70.6 %reduce-scatter.5.cloned.1.call-start = ((), (), s32[]{:S(2)}) async-start(), calls=%async_computation.5 | async-start | bytes 4587520 | tf_op jit(solution)/shard_map/reduce_scatter | solution.py:23
  7.2 23.0 %slice-start = ((s8[7340032]{0:T(1024)(128)(4,1)}), s8[4194304]{0:T(1024)(128)(4,1)S(1)}, s32[]{:S(2)}) async-start(s8[7340032]{0:T(1024)(128)(4,1)} %bitcast.37), calls=%async_computation.14 | async-start | bytes 8388608
  24.9 5.3 %slice-start.1 = ((s8[7340032]{0:T(1024)(128)(4,1)}), s8[3145728]{0:T(1024)(128)(4,1)S(1)}, s32[]{:S(2)}) async-start(s8[7340032]{0:T(1024)(128)(4,1)} %bitcast.37), calls=%async_computation.15 | async-start | bytes 6291456
  34.6 0.9 copy-start.3
  34.6 75.9 %reduce-scatter.9.cloned.1.call-start = ((), (), s32[]{:S(2)}) async-start(), calls=%async_computation.8 | async-start | bytes 2293760 | tf_op jit(solution)/shard_map/reduce_scatter | solution.py:48
  58.3 76.1 %all-gather.8.cloned.1.call-start = ((), (), s32[]{:S(2)}) async-start(), calls=%async_computation.9 | async-start | bytes 2293760 | tf_op jit(solution)/shard_map/all_gather | solution.py:58
  113.1 44.4 %all-gather.12.cloned.1.call-start = ((), (), s32[]{:S(2)}) async-start(), calls=%async_computation.11 | async-start | bytes 2293760 | tf_op jit(solution)/shard_map/all_gather | solution.py:59
  113.7 66.9 %all-gather.6.cloned.1.call-start = ((), (), s32[]{:S(2)}) async-start(), calls=%async_computation.6 | async-start | bytes 2293760 | tf_op jit(solution)/shard_map/all_gather | solution.py:38
  114.3 124.2 %all-gather.10.cloned.1.call-start = ((), (), s32[]{:S(2)}) async-start(), calls=%async_computation.10 | async-start | bytes 5505024 | tf_op jit(solution)/shard_map/all_gather | solution.py:73
  134.4 156.5 %all-gather.14.cloned.1.call-start = ((), (), s32[]{:S(2)}) async-start(), calls=%async_computation.12 | async-start | bytes 5505024 | tf_op jit(solution)/shard_map/all_gather | solution.py:74
  157.5 158.1 %reduce-scatter.7.cloned.1.call-start = ((), (), s32[]{:S(2)}) async-start(), calls=%async_computation.7 | async-start | bytes 655360 | tf_op jit(solution)/shard_map/reduce_scatter | solution.py:40
  180.6 6.7 %copy-start.2 = (bf16[256,3584]{1,0:T(8,128)(2,1)S(1)}, bf16[256,3584]{1,0:T(8,128)(2,1)}, u32[]{:S(2)}) copy-start(bf16[256,3584]{1,0:T(8,128)(2,1)} %all-gather.6.cloned.1.call-done) | copy-start | bytes 5505028
  187.2 218.0 %reduce-scatter.11.cloned.1.call-start = ((), (), s32[]{:S(2)}) async-start(), calls=%async_computation.13 | async-start | bytes 11010048 | tf_op jit(solution)/shard_map/reduce_scatter | solution.py:64
  238.4 2.8 copy-start
  290.8 2.8 copy-start.1
Sparse Core Ops, SparseCore 0:
  34.8 42.9 reduce-scatter.4
  80.9 29.6 reduce-scatter.8
  113.2 21.0 all-gather.7
  136.3 21.0 all-gather.11
  159.4 21.0 all-gather.5
  182.0 56.4 all-gather.9
  240.0 50.8 all-gather.13
  293.7 21.8 reduce-scatter.6
  318.4 86.7 reduce-scatter.10
where the time goes:
time: 412 us
  waiting for transfers between devices  287 us (70%)
  blocking collectives  51.3 us (12%)
  matrix products  33.8 us (8%)
  between operations  14 us (3%)
  local copies, waits for them, and re-layouts  13.1 us (3%)
  other arithmetic  11.9 us (3%)
    reduce_scatter x1, waiting for transfers between devices, per_device(): lax.psum_scatter(down_term.astype(jnp.bfloat16), 'depth', scatter_dimensi...  89.7 us
    all_gather x1, waiting for transfers between devices, per_device(): up_piece = lax.all_gather(d_up_rows, 'depth', axis=0, tiled=True)  39.4 us
    reduce_scatter x1, waiting for transfers between devices, per_device(): lax.psum_scatter(lax.dot_general(row_piece, w_down, COLS_CONTRACT, prefer...  31.5 us
    all_gather x1, waiting for transfers between devices, per_device(): gate_piece = lax.all_gather(d_gate_rows, 'depth', axis=0, tiled=True)  28.3 us
    all_gather x1, waiting for transfers between devices, per_device(): lax.all_gather(d_up, 'row', axis=0, tiled=True)  23.1 us
    all_gather x1, waiting for transfers between devices, per_device(): hidden_rows = lax.all_gather(hidden, 'row', axis=0, tiled=True)  23 us
    all_gather x1, waiting for transfers between devices, per_device(): lax.all_gather(d_gate, 'row', axis=0, tiled=True)  20 us
    reduce_scatter x1, waiting for transfers between devices, per_device(): lax.psum_scatter(jnp.concatenate([jnp.dot(row_piece, w_gate, preferred_el...  19.4 us
  transfers between devices with their start and end apart: 9, of which 9 were waited for; matrix products, arithmetic and copies ran while one was open for 11% of the time, Pallas kernels for 0%

commit v1 on v0

--- a/solution.py
+++ b/solution.py
@@ -5,6 +5,19 @@
 
 COLS_CONTRACT = (((1,), (1,)), ((), ()))
 ROWS_CONTRACT = (((0,), (0,)), ((), ()))
+
+
+def put_run(z):
+    num_devices = lax.axis_size("row")
+    oldest = sorted(((d, (d + 1) % num_devices) for d in range(num_devices)))
+    passed = z
+    column = [passed]
+    for c in tuple(range(1, num_devices)):
+        passed = lax.ppermute(passed, axis_name="row", perm=oldest)
+        column.insert(0, passed)
+    return jnp.roll(
+        jnp.concatenate(column, axis=0), shift=(lax.axis_index("row") + 1) * z.shape[0], axis=0
+    )
 
 
 def gate_grads(hidden_grad, gate_sum, up_sum):
@@ -35,7 +48,7 @@
     gate_sum = joined[:, :hid_width]
     up_sum = joined[:, hid_width:]
     hidden = (jax.nn.silu(gate_sum) * up_sum).astype(jnp.bfloat16)
-    hidden_rows = lax.all_gather(hidden, "row", axis=0, tiled=True)
+    hidden_rows = put_run(hidden)
     row_piece = hidden_rows
     mixed = lax.psum_scatter(
         jnp.dot(row_piece, w_down, preferred_element_type=jnp.float32).astype(jnp.bfloat16),

time: 412 us -> 393 us (0.954)
  waiting for transfers between devices: 287 us -> 261 us
  local copies, waits for them, and re-layouts: 13.1 us -> 19.5 us
    ppermute x0 -> x3, waiting for transfers between devices: none -> 31.7 us  [put_run(): passed = lax.ppermute(passed, axis_name='row', perm=oldest)]
    all_gather x1, waiting for transfers between devices: 23.1 us -> 0.01 us  [per_device(): lax.all_gather(d_up, 'row', axis=0, tiled=True)]
    all_gather x1 -> x0, waiting for transfers between devices: 23 us -> none  [per_device(): hidden_rows = lax.all_gather(hidden, 'row', axis=0, tiled=True)]
    all_gather x1, waiting for transfers between devices: 28.3 us -> 16.1 us  [per_device(): gate_piece = lax.all_gather(d_gate_rows, 'depth', axis=0, tiled=True)]
    unnamed x14 -> x19, local copies, waits for them, and re-layouts: 12.9 us -> 18.5 us
  transfers between devices with their start and end apart: 9 -> 11, of which waited for: 9 -> 10; matrix products, arithmetic and copies ran while one was open for 11% -> 14% of each run, Pallas kernels for 0% -> 0%
where the time goes in v1:
time: 393 us
  waiting for transfers between devices  261 us (66%)
  blocking collectives  50.7 us (13%)
  matrix products  35.4 us (9%)
  local copies, waits for them, and re-layouts  19.5 us (5%)
  between operations  14.2 us (4%)
  other arithmetic  11.8 us (3%)
    reduce_scatter x1, waiting for transfers between devices, per_device(): lax.psum_scatter(down_term.astype(jnp.bfloat16), 'depth', scatter_dimensi...  89.7 us
    all_gather x1, waiting for transfers between devices, per_device(): up_piece = lax.all_gather(d_up_rows, 'depth', axis=0, tiled=True)  39.2 us
    ppermute x3, waiting for transfers between devices, put_run(): passed = lax.ppermute(passed, axis_name='row', perm=oldest)  31.7 us
    reduce_scatter x1, waiting for transfers between devices, per_device(): lax.psum_scatter(lax.dot_general(row_piece, w_down, COLS_CONTRACT, prefer...  31.5 us
    all_gather x1, waiting for transfers between devices, per_device(): lax.all_gather(d_gate, 'row', axis=0, tiled=True)  20.6 us
    reduce_scatter x1, waiting for transfers between devices, per_device(): lax.psum_scatter(jnp.concatenate([jnp.dot(row_piece, w_gate, preferred_el...  19.4 us
    unnamed x19, local copies, waits for them, and re-layouts  18.5 us
    all_gather x1, blocking collectives, per_device(): token_rows = lax.all_gather(tokens, 'col', axis=0, tiled=True)  17.7 us
  transfers between devices with their start and end apart: 11, of which 10 were waited for; matrix products, arithmetic and copies ran while one was open for 14% of the time, Pallas kernels for 0%

profile of v1, /device:TPU:0, one launch (start us, length us, event | category | flops | bytes accessed | tf_op | source)
XLA Modules:
  0.0 392.9 jit_solution(6578446263304724114)
XLA Ops:
  7.2 0.0 reduce-scatter.5.cloned.1.call-start
  7.2 0.0 slice-start
  7.2 17.7 %all_gather.18 = bf16[256,1024]{1,0:T(8,128)(2,1)S(1)} all-gather(bf16[64,1024]{1,0:T(8,128)(2,1)} %param.5), channel_id=1, replica_groups=mesh['row'=4,'col'=4,'depth'=2] {'col'}, dimensions={0}, use_global_device_ids=true | all-gather | bytes 655360 | tf_op jit(solution)/shard_map/all_gather | solution.py:34
  24.9 0.0 slice-start.1
  24.9 5.3 %convolution_convert_fusion.6 = bf16[256,3584]{1,0:T(8,128)(2,1)S(1)} fusion(bf16[256,1024]{1,0:T(8,128)(2,1)S(1)} %all_gather.18, bf16[1024,3584]{1,0:T(8,128)(2,1)} %param.7), kind=kOutput, calls=%fused_computation.12 | convolution fusion | flops 1879965696 | bytes 9699328 | tf_op jit(solution)/shard_map/dot_general | solution.py:40
  30.2 0.0 slice-done
  30.2 0.0 slice-done.1
  30.3 2.1 convolution_convert_fusion.7
  32.4 2.3 pad_maximum_fusion
  34.6 0.0 reduce-scatter.5.cloned.1.call-update
  34.6 0.0 reduce-scatter.9.cloned.1.call-start
  34.7 0.8 copy-done.2
  35.5 16.2 %all_gather.19 = bf16[256,1024]{1,0:T(8,128)(2,1)S(1)} all-gather(bf16[64,1024]{1,0:T(8,128)(2,1)S(1)} %copy-done.2), channel_id=1, replica_groups=mesh['row'=4,'col'=4,'depth'=2] {'col'}, dimensions={0}, use_global_device_ids=true | all-gather | bytes 655360 | tf_op jit(solution)/shard_map/all_gather | solution.py:59
  51.8 6.5 %convolution_convert_fusion.5 = bf16[256,3584]{1,0:T(8,128)(2,1)} fusion(bf16[256,1024]{1,0:T(8,128)(2,1)S(1)} %all_gather.19, bf16[3584,1024]{1,0:T(8,128)(2,1)} %param.8), kind=kOutput, calls=%fused_computation.11 | convolution fusion | flops 1879965696 | bytes 9699328 | tf_op jit(solution)/shard_map/dot_general | solution.py:62
  58.3 0.0 reduce-scatter.9.cloned.1.call-update
  58.3 0.0 all-gather.5.cloned.1.call-start
  58.3 19.4 %reduce-scatter.5.cloned.1.call-done = bf16[64,7168]{1,0:T(8,128)(2,1)} async-done(((bf16[256,7168]{1,0:T(8,128)(2,1)}), bf16[64,7168]{1,0:T(8,128)(2,1)}) %reduce-scatter.5.cloned.1.call-update) | async-done | bytes 917520 | tf_op jit(solution)/shard_map/reduce_scatter | solution.py:36
  77.8 1.3 convert_element_type.67
  79.1 31.5 %reduce-scatter.9.cloned.1.call-done = bf16[64,3584]{1,0:T(8,128)(2,1)} async-done(((bf16[256,3584]{1,0:T(8,128)(2,1)}), bf16[64,3584]{1,0:T(8,128)(2,1)}) %reduce-scatter.9.cloned.1.call-update) | async-done | bytes 458768 | tf_op jit(solution)/shard_map/reduce_scatter | solution.py:61
  110.5 2.4 fusion.18
  113.0 0.0 all-gather.5.cloned.1.call-update
  113.0 0.0 all-gather.9.cloned.1.call-start
  113.0 0.5 all-gather.9.cloned.1.call-update
  113.6 0.0 all-gather.7.cloned.1.call-start
  113.6 20.6 %all-gather.5.cloned.1.call-done = bf16[256,3584]{1,0:T(8,128)(2,1)} async-done(((bf16[64,3584]{1,0:T(8,128)(2,1)}), bf16[256,3584]{1,0:T(8,128)(2,1)}) %all-gather.5.cloned.1.call-update) | async-done | bytes 1835024 | tf_op jit(solution)/shard_map/all_gather | solution.py:71
  134.2 0.0 all-gather.7.cloned.1.call-update
  134.3 0.0 all-gather.11.cloned.1.call-start
  134.3 0.3 collective-permute-start
  134.6 7.7 %collective-permute-done = bf16[64,3584]{1,0:T(8,128)(2,1)S(1)} collective-permute-done((bf16[64,3584]{1,0:T(8,128)(2,1)S(1)}, bf16[64,3584]{1,0:T(8,128)(2,1)S(1)}, u32[]{:S(2)}, u32[]{:S(2)}) %collective-permute-start) | collective-permute-done | bytes 458784 | tf_op jit(solution)/shard_map/ppermute | solution.py:16
  142.3 0.0 collective-permute-start.1
  142.3 16.1 %collective-permute-done.1 = bf16[64,3584]{1,0:T(8,128)(2,1)S(1)} collective-permute-done((bf16[64,3584]{1,0:T(8,128)(2,1)S(1)}, bf16[64,3584]{1,0:T(8,128)(2,1)S(1)}, u32[]{:S(2)}, u32[]{:S(2)}) %collective-permute-start.1) | collective-permute-done | bytes 458784 | tf_op jit(solution)/shard_map/ppermute | solution.py:16
  158.4 0.0 collective-permute-start.2
  158.4 7.9 %collective-permute-done.2 = bf16[64,3584]{1,0:T(8,128)(2,1)S(1)} collective-permute-done((bf16[64,3584]{1,0:T(8,128)(2,1)S(1)}, bf16[64,3584]{1,0:T(8,128)(2,1)S(1)}, u32[]{:S(2)}, u32[]{:S(2)}) %collective-permute-start.2) | collective-permute-done | bytes 458784 | tf_op jit(solution)/shard_map/ppermute | solution.py:16
  166.3 0.8 constant_dynamic-update-slice_fusion.7
  167.1 0.0 all-gather.11.cloned.1.call-update
  167.1 0.0 reduce-scatter.7.cloned.1.call-start
  167.1 0.8 constant_dynamic-update-slice_fusion.6
  167.9 0.8 constant_dynamic-update-slice_fusion.5
  168.7 0.8 constant_dynamic-update-slice_fusion.4
  169.5 0.8 constant_dynamic-update-slice_fusion.3
  170.3 0.8 constant_dynamic-update-slice_fusion.2
  171.1 0.8 constant_dynamic-update-slice_fusion.1
  171.9 0.8 constant_dynamic-update-slice_fusion
  172.7 7.0 %fusion.11 = bf16[256,1024]{1,0:T(8,128)(2,1)} fusion(bf16[3584,1024]{1,0:T(8,128)(2,1)} %param.8, bf16[512,3584]{1,0:T(8,128)(2,1)} %constant_dynamic-update-slice_fusion, s32[]{:T(128)S(6)} %select_n.14), kind=kOutput, calls=%fused_computation.22 | convolution fusion | flops 1879310336 | bytes 9699332 | tf_op jit(solution)/shard_map/dot_general | solution.py:54
  179.7 0.0 reduce-scatter.7.cloned.1.call-update
  179.7 0.0 reduce-scatter.11.cloned.1.call-start
  179.8 6.6 %convolution_convert_fusion = bf16[3584,1024]{1,0:T(8,128)(2,1)} fusion(bf16[256,1024]{1,0:T(8,128)(2,1)S(1)} %all_gather.19, bf16[512,3584]{1,0:T(8,128)(2,1)} %constant_dynamic-update-slice_fusion, s32[]{:T(128)S(6)} %select_n.14), kind=kOutput, calls=%fused_computation | convolution fusion | flops 1882718208 | bytes 9699332 | tf_op jit(solution)/shard_map/dot_general | solution.py:74
  186.4 0.0 reduce-scatter.11.cloned.1.call-update
  186.4 0.2 copy.18
  186.6 16.8 %all_to_all.16 = bf16[256,2,512]{0,2,1:T(8,128)(2,1)S(1)} all-to-all(bf16[256,2,512]{0,2,1:T(8,128)(2,1)S(1)} %bitcast.34), channel_id=1, replica_groups=mesh['row'=4,'col'=4,'depth'=2] {'depth'}, dimensions={1} | all-to-all | bytes 1048576 | tf_op jit(solution)/shard_map/all_to_all | solution.py:80
  203.3 16.1 %all-gather.7.cloned.1.call-done = bf16[512,3584]{1,0:T(8,128)(2,1)} async-done(((bf16[256,3584]{1,0:T(8,128)(2,1)}), bf16[512,3584]{1,0:T(8,128)(2,1)}) %all-gather.7.cloned.1.call-update) | async-done | bytes 3670032 | tf_op jit(solution)/shard_map/all_gather | solution.py:86
  219.4 2.8 fusion
  222.2 0.0 copy-done
  222.2 1.2 fusion.1
  223.4 2.9 add_convert_fusion.1
  226.3 6.2 %copy.21 = bf16[512,3584]{1,0:T(8,128)(2,1)} copy(bf16[512,3584]{0,1:T(8,128)(2,1)} %add_convert_fusion.1) | data formatting | bytes 7340032
  232.4 39.2 %all-gather.11.cloned.1.call-done = bf16[512,3584]{1,0:T(8,128)(2,1)} async-done(((bf16[256,3584]{1,0:T(8,128)(2,1)}), bf16[512,3584]{1,0:T(8,128)(2,1)}) %all-gather.11.cloned.1.call-update) | async-done | bytes 3670032 | tf_op jit(solution)/shard_map/all_gather | solution.py:87
  271.6 2.8 fusion.2
  274.5 0.0 copy-done.1
  274.5 1.2 fusion.3
  275.7 3.0 add_convert_fusion
  278.6 5.9 %copy.22 = bf16[512,3584]{1,0:T(8,128)(2,1)} copy(bf16[512,3584]{0,1:T(8,128)(2,1)} %add_convert_fusion) | data formatting | bytes 7340032
  284.5 11.8 %reduce-scatter.7.cloned.1.call-done = bf16[64,1024]{1,0:T(8,128)(2,1)} async-done(((bf16[256,1024]{1,0:T(8,128)(2,1)}), bf16[64,1024]{1,0:T(8,128)(2,1)}) %reduce-scatter.7.cloned.1.call-update) | async-done | bytes 131088 | tf_op jit(solution)/shard_map/reduce_scatter | solution.py:53
  296.3 89.7 %reduce-scatter.11.cloned.1.call-done = bf16[1792,1024]{1,0:T(8,128)(2,1)} async-done(((bf16[3584,1024]{1,0:T(8,128)(2,1)}), bf16[1792,1024]{1,0:T(8,128)(2,1)}) %reduce-scatter.11.cloned.1.call-update) | async-done | bytes 3670032 | tf_op jit(solution)/shard_map/reduce_scatter | solution.py:77
  (5 shorter events, 0.0 us)
Async XLA Ops:
  7.2 70.6 %reduce-scatter.5.cloned.1.call-start = ((), (), s32[]{:S(2)}) async-start(), calls=%async_computation.5 | async-start | bytes 4587520 | tf_op jit(solution)/shard_map/reduce_scatter | solution.py:36
  7.2 23.0 %slice-start = ((s8[7340032]{0:T(1024)(128)(4,1)}), s8[4194304]{0:T(1024)(128)(4,1)S(1)}, s32[]{:S(2)}) async-start(s8[7340032]{0:T(1024)(128)(4,1)} %bitcast.35), calls=%async_computation.13 | async-start | bytes 8388608
  24.9 5.3 %slice-start.1 = ((s8[7340032]{0:T(1024)(128)(4,1)}), s8[3145728]{0:T(1024)(128)(4,1)S(1)}, s32[]{:S(2)}) async-start(s8[7340032]{0:T(1024)(128)(4,1)} %bitcast.35), calls=%async_computation.14 | async-start | bytes 6291456
  34.6 0.9 copy-start.2
  34.6 75.9 %reduce-scatter.9.cloned.1.call-start = ((), (), s32[]{:S(2)}) async-start(), calls=%async_computation.7 | async-start | bytes 2293760 | tf_op jit(solution)/shard_map/reduce_scatter | solution.py:61
  58.3 76.0 %all-gather.5.cloned.1.call-start = ((), (), s32[]{:S(2)}) async-start(), calls=%async_computation.8 | async-start | bytes 2293760 | tf_op jit(solution)/shard_map/all_gather | solution.py:71
  113.0 54.1 %all-gather.9.cloned.1.call-start = ((), (), s32[]{:S(2)}) async-start(), calls=%async_computation.10 | async-start | bytes 2293760 | tf_op jit(solution)/shard_map/all_gather | solution.py:72
  113.6 105.8 %all-gather.7.cloned.1.call-start = ((), (), s32[]{:S(2)}) async-start(), calls=%async_computation.9 | async-start | bytes 5505024 | tf_op jit(solution)/shard_map/all_gather | solution.py:86
  134.3 137.4 %all-gather.11.cloned.1.call-start = ((), (), s32[]{:S(2)}) async-start(), calls=%async_computation.11 | async-start | bytes 5505024 | tf_op jit(solution)/shard_map/all_gather | solution.py:87
  134.3 8.0 %collective-permute-start = (bf16[64,3584]{1,0:T(8,128)(2,1)S(1)}, bf16[64,3584]{1,0:T(8,128)(2,1)S(1)}, u32[]{:S(2)}, u32[]{:S(2)}) collective-permute-start(bf16[64,3584]{1,0:T(8,128)(2,1)S(1)} %get-tuple-element.22), channel_id=1, source_target_pairs={{0,8},{8,16},{16,24},{24,0},{1,9},{9,17},{17,25},{25,1},{2,10},{10... | collective-permute-start | bytes 1376264 | tf_op jit(solution)/shard_map/ppermute | solution.py:16
  142.3 16.1 %collective-permute-start.1 = (bf16[64,3584]{1,0:T(8,128)(2,1)S(1)}, bf16[64,3584]{1,0:T(8,128)(2,1)S(1)}, u32[]{:S(2)}, u32[]{:S(2)}) collective-permute-start(bf16[64,3584]{1,0:T(8,128)(2,1)S(1)} %collective-permute-done), channel_id=1, source_target_pairs={{0,8},{8,16},{16,24},{24,0},{1,9},{9,17},{17,25},{25,1},{2,10},{10... | collective-permute-start | bytes 1376264 | tf_op jit(solution)/shard_map/ppermute | solution.py:16
  158.4 7.9 %collective-permute-start.2 = (bf16[64,3584]{1,0:T(8,128)(2,1)S(1)}, bf16[64,3584]{1,0:T(8,128)(2,1)S(1)}, u32[]{:S(2)}, u32[]{:S(2)}) collective-permute-start(bf16[64,3584]{1,0:T(8,128)(2,1)S(1)} %collective-permute-done.1), channel_id=1, source_target_pairs={{0,8},{8,16},{16,24},{24,0},{1,9},{9,17},{17,25},{25,1},{2,10},{10... | collective-permute-start | bytes 1376264 | tf_op jit(solution)/shard_map/ppermute | solution.py:16
  167.1 129.3 %reduce-scatter.7.cloned.1.call-start = ((), (), s32[]{:S(2)}) async-start(), calls=%async_computation.6 | async-start | bytes 655360 | tf_op jit(solution)/shard_map/reduce_scatter | solution.py:53
  179.7 206.3 %reduce-scatter.11.cloned.1.call-start = ((), (), s32[]{:S(2)}) async-start(), calls=%async_computation.12 | async-start | bytes 11010048 | tf_op jit(solution)/shard_map/reduce_scatter | solution.py:77
  219.4 2.8 copy-start
  271.6 2.8 copy-start.1
Sparse Core Ops, SparseCore 0:
  34.8 42.9 reduce-scatter.4
  80.9 29.6 reduce-scatter.8
  113.1 21.0 all-gather.4
  136.2 25.2 all-gather.8
  162.9 56.4 all-gather.6
  220.8 50.8 all-gather.10
  274.5 21.8 reduce-scatter.6
  299.2 86.7 reduce-scatter.10
